TPU v7x, 256 devices: a whole 4x4x8 slice. The times are simulated.
256 devices in a mesh: row: 32 (over y, z_hi, core), col: 8 (over z_lo, x).
Axes of the slice: x: 4, y: 4, z: 8 (z_hi: 4, z_lo: 2; z = z_hi * 2 + z_lo), core: 2. Of those that a mesh axis runs over, the one named last changes fastest.
Arguments:
- alignment: bfloat16 [64, 1024, 64], P(None, ('col', 'row')), may hold values from -6 to 6
- pair_rep: bfloat16 [1024, 1024, 128], P('row', 'col'), may hold values from -128 to 128
- outer_left: bfloat16 [64, 32], replicated, may hold values from -0.75 to 0.75
- outer_right: bfloat16 [64, 32], replicated, may hold values from -0.75 to 0.75
- outer_proj: bfloat16 [1024, 128], replicated, may hold values from -1.5 to 1.5
- outer_bias: float32 [128], replicated, may hold values from -3 to 3
- average_value: bfloat16 [64, 256], replicated, may hold values from -0.75 to 0.75
- average_gate: bfloat16 [64, 256], replicated, may hold values from -0.75 to 0.75
- average_logit: bfloat16 [128, 8], replicated, may hold values from -28 to 28
- average_out: bfloat16 [256, 64], replicated, may hold values from -1 to 1
- triangle_proj: bfloat16 [128, 512], replicated, may hold values from -0.5 to 0.5
- triangle_bias: bfloat16 [128, 4], replicated, may hold values from -0.5 to 0.5
Outputs:
- pair_new: bfloat16 [1024, 1024, 128], P('row', 'col')
- alignment_update: bfloat16 [64, 1024, 64], P(None, ('row', 'col'))
- triangle_inputs: bfloat16 [1024, 1024, 512], P(('col', 'row'))
- edge_bias: bfloat16 [4, 1024, 1024], P(None, ('col', 'row'))
All inputs are finite; a program needn't handle non-finite values.
Results may differ from a plain program's by a relative error of at most 0.02.
The roundings to bfloat16 on the way count: a program that leaves them out, or rounds other values in their place, can miss the bound.
Values may be sent and summed in bfloat16 or wider, within the bound.
No kernel may reach another device: no remote copies, remote signals or barrier semaphores. Data moves between devices by JAX's collectives and lax.ppermute only.
A program may use at most 64 MiB of HBM per device.

v0:
```python
import functools

import jax
import jax.numpy as jnp
from jax import lax
from jax.experimental import pallas as pl
from jax.experimental.pallas import tpu as pltpu
from jax.sharding import Mesh, PartitionSpec as P


BF16 = jnp.bfloat16
F32 = jnp.float32
ROW = ("y", "zh", "co")
COL = ("zl", "x")
ALL = ROW + COL


def dot(a, b):
    return jnp.dot(a, b, preferred_element_type=F32)


def dot_nt(a, b):
    return lax.dot_general(a, b, (((1,), (1,)), ((), ())), preferred_element_type=F32)


def cost(flops, nbytes, trans=0):
    return pl.CostEstimate(flops=flops, bytes_accessed=nbytes, transcendentals=trans)


def standardize(values):
    widened = values.astype(F32)
    centered = widened - jnp.mean(widened, axis=-1, keepdims=True)
    spread = jnp.mean(centered * centered, axis=-1, keepdims=True)
    return centered * lax.rsqrt(spread + 1e-05)


def iota(shape, dim):
    return lax.broadcasted_iota(jnp.int32, shape, dim)


def picker(rows, cols, rule):
    return jnp.where(rule(iota((rows, cols), 0), iota((rows, cols), 1)), 1.0, 0.0).astype(BF16)


def banded(wide, copies, col_period, col_width):
    tall = jnp.concatenate([wide] * copies, axis=0)
    rows, cols = tall.shape
    here = iota((rows, cols), 0) // wide.shape[0]
    there = (iota((rows, cols), 1) % col_period) // col_width
    return jnp.where(here == there, tall, 0.0).astype(BF16)


def prep_kernel(align_ref, left_ref, out_ref, wide, plane):
    wide[...] = align_ref[...].astype(F32)
    lefts = []
    for t in range(4):
        normed = standardize(wide[:, t, :]).astype(BF16)
        plane[...] = normed.astype(F32)
        out_ref[t * 32 : (t + 1) * 32, :] = jnp.concatenate(
            [plane[pl.ds(0, 32, stride=2), :], plane[pl.ds(1, 32, stride=2), :]], axis=1
        ).astype(BF16)
        lefts.append(dot_nt(normed, left_ref[...]))
    out_ref[128:192, :] = jnp.concatenate(lefts, axis=1).astype(BF16)


def prep_stage(alignment, outer_left):
    return pl.pallas_call(
        prep_kernel,
        out_shape=jax.ShapeDtypeStruct((192, 128), BF16),
        scratch_shapes=[pltpu.VMEM((64, 4, 64), F32), pltpu.VMEM((64, 64), F32)],
        cost_estimate=cost(10_000_000, 100_000),
        compiler_params=pltpu.CompilerParams(vmem_limit_bytes=4 * 2**20),
        name="prep_stage",
    )(alignment, outer_left)


def right_kernel(near_ref, right_ref, out_ref, norm_ref, wide, tall):
    norms = near_ref[:, :128, :]
    norm_ref[...] = norms
    wide[...] = norms.reshape(1024, 128).astype(F32)
    rows = dot(picker(256, 32, lambda r, c: r // 8 == c), right_ref[...]).astype(BF16)
    rows = dot(rows, picker(64, 512, lambda r, c: c % 64 == r))
    here = iota((256, 512), 0) % 8
    there = iota((256, 512), 1) // 64
    weights = jnp.where(here == there, rows, 0.0).astype(BF16)
    for g in range(8):
        cols = jnp.concatenate(
            [wide[pl.ds(4 * g + k, 32, stride=32), :] for k in range(4)], axis=1
        ).astype(BF16)
        tall[g] = dot_nt(weights, cols)
    for g in range(8):
        group = jnp.concatenate(
            [
                tall[k, (g * 4 + d) * 8 : (g * 4 + d + 1) * 8, :]
                for d in range(4)
                for k in range(8)
            ],
            axis=0,
        )
        out_ref[g] = jnp.transpose(group).astype(BF16)


def right_stage(near, right_w):
    return pl.pallas_call(
        right_kernel,
        in_specs=[pl.BlockSpec(memory_space=pltpu.VMEM)] * 2,
        out_shape=[
            jax.ShapeDtypeStruct((8, 32, 256), BF16),
            jax.ShapeDtypeStruct((8, 128, 128), BF16),
        ],
        scratch_shapes=[pltpu.VMEM((1024, 128), F32), pltpu.VMEM((8, 256, 32), F32)],
        cost_estimate=cost(500_000_000, 500_000),
        compiler_params=pltpu.CompilerParams(vmem_limit_bytes=8 * 2**20),
        name="right_stage",
    )(near, right_w)


def pair_kernel(
    right_ref, left_ref, pair_ref, proj_ref, bias_ref, logit_w_ref,
    new_ref, turned_ref, logit_ref,
    stack, proj, tall, plane, turn,
):
    rows = pair_ref.shape[0]

    @pl.when(pl.program_id(0) == 0)
    def _():
        for g in range(8):
            for y in range(4):
                start = g * 128 + y * 32
                stack[start : start + 32, :] = right_ref[y, g]
        tall[...] = proj_ref[...].astype(F32)
        for d in range(32):
            proj[d * 32 : (d + 1) * 32, :] = tall[pl.ds(d, 32, stride=32), :].astype(BF16)

    for quad in range(rows // 4):
        outer_rows = []
        for p in range(2):
            choose = picker(
                128, 256, lambda r, c: (r // 32 == 2 * p + c // 128) & (r % 32 == c % 32)
            )
            wide = dot(left_ref[quad * 64 : (quad + 1) * 64, :], choose)
            outer = dot(stack[...], banded(wide, 4, 128, 32)).astype(BF16)
            for k in range(2):
                outer_rows.append(
                    jnp.concatenate(
                        [
                            outer[g * 128 : (g + 1) * 128, k * 128 : (k + 1) * 128]
                            for g in range(8)
                        ],
                        axis=1,
                    )
                )
        update = dot(jnp.concatenate(outer_rows, axis=0), proj[...])
        four = slice(quad * 4, (quad + 1) * 4)
        pair = pair_ref[four].reshape(512, 128).astype(F32)
        fresh = (pair + update * (1.0 / 64.0) + bias_ref[...]).astype(BF16)
        new_ref[four] = fresh.reshape(4, 128, 128)
        normed = standardize(fresh)
        normed_low = normed.astype(BF16)
        for i in range(4):
            logit_ref[quad * 4 + i] = dot_nt(
                logit_w_ref[...], normed_low[i * 128 : (i + 1) * 128]
            )
        plane[quad] = normed
        for i in range(4):
            for q in range(4):
                turn[pl.ds((quad * 4 + i) * 4 + q, 32, stride=4 * rows), :] = plane[
                    quad, pl.ds(i * 128 + q, 32, stride=4), :
                ]
    turned_ref[...] = turn[...].reshape(32, 4 * rows, 128).astype(BF16)


def pair_stage(right, left, pair_rep, proj, bias, logit_w):
    block = 8
    steps = 32 // block
    return pl.pallas_call(
        pair_kernel,
        grid=(steps,),
        in_specs=[
            pl.BlockSpec((4, 8, 32, 256), lambda b: (0, 0, 0, 0)),
            pl.BlockSpec((16 * block, 128), lambda b: (b, 0)),
            pl.BlockSpec((block, 128, 128), lambda b: (b, 0, 0)),
            pl.BlockSpec((1024, 128), lambda b: (0, 0)),
            pl.BlockSpec((1, 128), lambda b: (0, 0)),
            pl.BlockSpec((8, 128), lambda b: (0, 0)),
        ],
        out_specs=[
            pl.BlockSpec((block, 128, 128), lambda b: (b, 0, 0)),
            pl.BlockSpec((32, 4 * block, 128), lambda b: (0, b, 0)),
            pl.BlockSpec((block, 8, 128), lambda b: (b, 0, 0)),
        ],
        out_shape=[
            jax.ShapeDtypeStruct((32, 128, 128), BF16),
            jax.ShapeDtypeStruct((32, 128, 128), BF16),
            jax.ShapeDtypeStruct((32, 8, 128), F32),
        ],
        scratch_shapes=[
            pltpu.VMEM((1024, 256), BF16),
            pltpu.VMEM((1024, 128), BF16),
            pltpu.VMEM((1024, 128), F32),
            pltpu.VMEM((block // 4, 512, 128), F32),
            pltpu.VMEM((block * 128, 128), F32),
        ],
        cost_estimate=cost(8_000_000_000, 6_000_000),
        compiler_params=pltpu.CompilerParams(vmem_limit_bytes=26 * 2**20),
        name="pair_stage",
    )(right, left, pair_rep, proj, bias, logit_w)


def by_heads():
    return picker(256, 1024, lambda r, c: (r // 32 == c // 128) & (r % 32 == c % 32))


def pack_stats(denom, peak):
    high = denom.astype(BF16).astype(F32)
    lane = iota((denom.shape[0], 128), 1)
    return jnp.where(
        lane == 0,
        high,
        jnp.where(lane == 1, denom - high, jnp.where(lane == 2, peak, 0.0)),
    )


def average_kernel(me_ref, logit_ref, value_ref, *refs):
    norms, outs, (wide, spare, summed, parts) = refs[:4], refs[4:8], refs[8:]
    me_y, me_z, me_x = me_ref[0], me_ref[1], me_ref[2]
    logits = logit_ref[...].reshape(256, 128)
    peak = jnp.max(logits, axis=1, keepdims=True).astype(BF16).astype(F32)
    weights = jnp.exp(logits - peak).astype(BF16).astype(F32)
    stats = pack_stats(jnp.sum(weights, axis=1, keepdims=True), peak)
    spare[...] = weights
    by_head = jnp.concatenate(
        [spare[pl.ds(h, 32, stride=8), :] for h in range(8)], axis=0
    ).astype(BF16)
    for s in range(4):
        start = pl.multiple_of(lax.rem(me_y + 4 - s, 4) * 1024, 1024)
        wide[pl.ds(start, 1024), :] = norms[s][...].reshape(1024, 128).astype(F32)
    for g in range(16):
        cols = jnp.concatenate(
            [wide[pl.ds(2 * g + k, 128, stride=32), :] for k in range(2)], axis=1
        ).astype(BF16)
        summed[g] = dot(by_head, cols).astype(BF16)
    spare[...] = stats
    targets = [
        [lax.rem(me_z + k, 2) * 4 + lax.rem(me_x + s, 4) for k in range(2)] for s in range(4)
    ]
    for s in range(4):
        for k in range(2):
            start = pl.multiple_of(targets[s][k] * 32, 32)
            outs[s][k, 512:544, :] = spare[pl.ds(start, 32), :].astype(BF16)
    value_w = banded(dot(value_ref[...], by_heads()), 4, 128, 32)
    for h in range(8):
        rows = summed[:, h * 32 : (h + 1) * 32, :].reshape(512, 256)
        parts[...] = dot(rows, value_w[:, h * 128 : (h + 1) * 128])
        for s in range(4):
            for k in range(2):
                for i in range(4):
                    start = h * 64 + i * 16
                    outs[s][k, start : start + 16, :] = parts[
                        pl.ds(targets[s][k] * 4 + i, 16, stride=32), :
                    ].astype(BF16)


def average_stage(me, logits, value, norms):
    return pl.pallas_call(
        average_kernel,
        in_specs=[
            pl.BlockSpec(memory_space=pltpu.SMEM),
        ]
        + [pl.BlockSpec(memory_space=pltpu.VMEM)] * 6,
        out_shape=[jax.ShapeDtypeStruct((2, 544, 128), BF16)] * 4,
        scratch_shapes=[
            pltpu.VMEM((4096, 128), F32),
            pltpu.VMEM((256, 128), F32),
            pltpu.VMEM((16, 256, 256), BF16),
            pltpu.VMEM((512, 128), F32),
        ],
        cost_estimate=cost(2_000_000_000, 3_000_000),
        compiler_params=pltpu.CompilerParams(vmem_limit_bytes=16 * 2**20),
        name="average_stage",
    )(me, logits, value, *norms)


def merge_stats(stats):
    denoms = [st[:, 0:1] + st[:, 1:2] for st in stats]
    peaks = [st[:, 2:3] for st in stats]
    top = functools.reduce(jnp.maximum, peaks)
    scales = [jnp.exp(peak - top) for peak in peaks]
    denom = functools.reduce(jnp.add, [s * d for s, d in zip(scales, denoms)])
    return top, scales, denom


def head_rows(factor, h):
    return jnp.concatenate(
        [jnp.broadcast_to(factor[i * 8 + h : i * 8 + h + 1], (16, 128)) for i in range(4)],
        axis=0,
    )


def merge_kernel(a_ref, b_ref, c_ref, d_ref, keep_ref, send_ref):
    sources = (a_ref, b_ref, c_ref, d_ref)
    for k, out in ((1, send_ref), (0, keep_ref)):
        top, scales, denom = merge_stats([r[k, 512:544, :].astype(F32) for r in sources])
        out[512:544, :] = pack_stats(denom, top).astype(out.dtype)
        factors = [jnp.broadcast_to(s, (32, 128)) for s in scales]
        for h in range(8):
            span = slice(h * 64, (h + 1) * 64)
            terms = [
                r[k, span, :].astype(F32) * head_rows(f, h) for r, f in zip(sources, factors)
            ]
            out[span, :] = ((terms[0] + terms[1]) + (terms[2] + terms[3])).astype(out.dtype)


def merge_stage(parts):
    return pl.pallas_call(
        merge_kernel,
        in_specs=[pl.BlockSpec(memory_space=pltpu.VMEM)] * 4,
        out_shape=[
            jax.ShapeDtypeStruct((544, 128), F32),
            jax.ShapeDtypeStruct((544, 128), BF16),
        ],
        cost_estimate=cost(10_000_000, 2_000_000),
        compiler_params=pltpu.CompilerParams(vmem_limit_bytes=6 * 2**20),
        name="merge_stage",
    )(*parts)


def combine_kernel(
    kept_ref, got_ref, norm_ref, gate_ref, proj_ref, out_ref, plane, placed
):
    parts = (kept_ref, got_ref)
    _, scales, denom = merge_stats([r[512:544, :].astype(F32) for r in parts])
    factors = [jnp.broadcast_to(s / denom, (32, 128)) for s in scales]
    plane[...] = norm_ref[...].astype(F32)
    norms = jnp.concatenate(
        [plane[pl.ds(k, 64, stride=2), :] for k in range(2)], axis=1
    ).astype(BF16)
    gate_w = banded(dot(gate_ref[...], by_heads()), 4, 128, 32)
    gate = jax.nn.sigmoid(dot(norms, gate_w))
    proj_w = banded(dot(proj_ref[...], by_heads()), 4, 128, 32)
    total_out = None
    for h in range(8):
        span = slice(h * 64, (h + 1) * 64)
        total = functools.reduce(
            jnp.add,
            [r[span, :].astype(F32) * head_rows(f, h) for r, f in zip(parts, factors)],
        )
        gated = total * gate[:, h * 128 : (h + 1) * 128]
        proj = proj_w[:, h * 128 : (h + 1) * 128]
        high = gated.astype(BF16)
        rest = gated - high.astype(F32)
        middle = rest.astype(BF16)
        low = (rest - middle.astype(F32)).astype(BF16)
        term = dot_nt(low, proj) + dot_nt(middle, proj) + dot_nt(high, proj)
        total_out = term if total_out is None else total_out + term
    for i in range(4):
        for k in range(4):
            placed[pl.ds(k, 16, stride=4), i, :] = total_out[
                i * 16 : (i + 1) * 16, k * 64 : (k + 1) * 64
            ]
    out_ref[...] = placed[...].astype(BF16)


def combine_stage(kept, got, norms, gate, proj):
    return pl.pallas_call(
        combine_kernel,
        in_specs=[pl.BlockSpec(memory_space=pltpu.VMEM)] * 5,
        out_shape=jax.ShapeDtypeStruct((64, 4, 64), BF16),
        scratch_shapes=[pltpu.VMEM((128, 128), F32), pltpu.VMEM((64, 4, 64), F32)],
        cost_estimate=cost(300_000_000, 2_500_000),
        compiler_params=pltpu.CompilerParams(vmem_limit_bytes=10 * 2**20),
        name="combine_stage",
    )(kept, got, norms, gate, proj)


def triangle_kernel(turned_ref, proj_ref, bias_ref, inputs_ref, edge_ref, plane):
    start = pl.program_id(0) * 4
    plane[...] = turned_ref[pl.ds(start, 4)].reshape(512, 128).astype(F32)
    for q in range(4):
        rows = jnp.concatenate(
            [plane[pl.ds(p * 128 + q, 32, stride=4), :] for p in range(4)], axis=0
        ).astype(BF16)
        projected = dot(rows, proj_ref[...])
        inputs_ref[q, :, :384] = projected[:, :384].astype(BF16)
        inputs_ref[q, :, 384:] = jax.nn.sigmoid(projected[:, 384:]).astype(BF16)
        edge_ref[:, q, :] = dot_nt(bias_ref[...], rows).astype(BF16)


def triangle_stage(turned, proj, bias):
    return pl.pallas_call(
        triangle_kernel,
        grid=(8,),
        in_specs=[
            pl.BlockSpec(memory_space=pltpu.VMEM),
            pl.BlockSpec((128, 512), lambda b: (0, 0)),
            pl.BlockSpec((4, 128), lambda b: (0, 0)),
        ],
        out_specs=[
            pl.BlockSpec((4, 128, 512), lambda b: (0, b, 0)),
            pl.BlockSpec((4, 4, 128), lambda b: (0, 0, b)),
        ],
        out_shape=[
            jax.ShapeDtypeStruct((4, 1024, 512), BF16),
            jax.ShapeDtypeStruct((4, 4, 1024), BF16),
        ],
        scratch_shapes=[pltpu.VMEM((512, 128), F32)],
        cost_estimate=cost(1_000_000_000, 6_000_000),
        compiler_params=pltpu.CompilerParams(vmem_limit_bytes=10 * 2**20),
        name="triangle_stage",
    )(turned, proj, bias)


ROUTES = (
    0o71546320, 0o60213574, 0o71453620, 0o46231075, 0o54762013, 0o13207546, 0o64750132, 0o31027654,
    0o02675431, 0o51034276, 0o02647135, 0o70132564, 0o67541302, 0o20316475, 0o57643210, 0o20315467,
    0o12603547, 0o14570236, 0o31607452, 0o46752013, 0o31654720, 0o64302157, 0o20456713, 0o57230146,
    0o32716450, 0o70463125, 0o20135467, 0o57642301, 0o02745631, 0o75210364, 0o13674520, 0o64012357,
)


def left_pairs():
    pairs = []
    for y in range(4):
        for c in range(8):
            route = ROUTES[y * 8 + c]
            for k in range(8):
                target = (route >> (3 * (7 - k))) % 8
                pairs.append(((y * 8 + k) * 8 + c, (c * 4 + y) * 8 + target))
    return pairs


def row_pairs():
    pairs = []
    for r in range(32):
        for c in range(8):
            pairs.append((r * 8 + c, (c * 4 + r // 8) * 8 + r % 8))
    return pairs


def per_device(
    alignment, pair_rep, outer_left, outer_right, outer_proj, outer_bias,
    average_value, average_gate, average_logit, average_out, triangle_proj, triangle_bias,
):
    me = jnp.stack([lax.axis_index(a) for a in ("y", "zl", "x")]).astype(jnp.int32)
    own = prep_stage(alignment, jnp.transpose(outer_left))
    near = lax.all_gather(own, ("zh", "co"), axis=0)
    left_rows = lax.ppermute(near[:, 128:].reshape(512, 128), ALL, left_pairs())
    right, near_norm = right_stage(near, jnp.transpose(outer_right))
    right = lax.all_gather(right, "y", axis=0)
    near_norm, right = lax.optimization_barrier((near_norm, right))
    norm_cols = [near_norm] + [
        lax.ppermute(near_norm, "y", [(c, (c + s) % 4) for c in range(4)])
        for s in range(1, 4)
    ]
    pair_new, turned, logits = pair_stage(
        right, left_rows, pair_rep, outer_proj,
        outer_bias.reshape(1, 128), jnp.transpose(average_logit),
    )
    turned = lax.all_to_all(turned, ROW, 0, 0, tiled=True)
    parts = average_stage(me, logits, average_value, norm_cols)
    moved = {}
    for s in (2, 1, 3):
        moved[s] = lax.ppermute(parts[s], "x", [(c, (c + s) % 4) for c in range(4)])
    norm_own = lax.ppermute(own[:128], ALL, row_pairs())
    kept, sent = merge_stage([parts[0], moved[1], moved[2], moved[3]])
    got = lax.ppermute(sent, "zl", [(0, 1), (1, 0)])
    alignment_update = combine_stage(
        kept, got, norm_own, average_gate, jnp.transpose(average_out)
    )
    turned, alignment_update = lax.optimization_barrier((turned, alignment_update))
    triangle_inputs, edge_bias = triangle_stage(
        turned, triangle_proj, jnp.transpose(triangle_bias)
    )
    return (pair_new, alignment_update, triangle_inputs, edge_bias)


def solution(mesh):
    fine = Mesh(mesh.devices.reshape(4, 4, 2, 2, 4), ALL)
    placed = (P(None, COL + ROW, None), P(ROW, COL, None)) + (P(),) * 10
    return jax.shard_map(
        per_device,
        mesh=fine,
        in_specs=placed,
        out_specs=(
            P(ROW, COL, None),
            P(None, ROW + COL, None),
            P(COL + ROW, None, None),
            P(None, COL + ROW, None),
        ),
        check_vma=False,
    )
```

profile of v0, /device:TPU:56, one launch (start us, length us, event | category | flops | bytes accessed | tf_op | source)
XLA Modules:
  0.0 134.6 jit_solution(6150423167561780568)
XLA Ops:
  0.6 0.8 copy-done
  1.5 0.7 copy-done.1
  2.2 0.5 prep_stage.1
  2.6 17.5 %all-gather = bf16[1536,128]{1,0:T(8,128)(2,1)S(1)} all-gather(bf16[192,128]{1,0:T(8,128)(2,1)S(1)} %prep_stage.1), channel_id=2, replica_groups=mesh['y'=4,'zh'=4,'co'=2,'zl'=2,'x'=4] {'zh','co'}, dimensions={0}, use_global_device_ids=true | all-gather | bytes 442368 | tf_op jit(solution)/shard_map/all_gather | solution.py:446
  20.2 3.1 %collective-permute-start = (bf16[512,128]{1,0:T(8,128)(2,1)S(1)}, bf16[512,128]{1,0:T(8,128)(2,1)S(1)}, u32[]{:S(2)}, u32[]{:S(2)}) collective-permute-start(bf16[512,128]{1,0:T(8,128)(2,1)S(1)} %bitcast.21), channel_id=1, source_target_pairs={{0,7},{8,1},{16,5},{24,4},{32,6},{40,3},{48,2},{56,0},{1,38},{9,32... | collective-permute-start | bytes 393224 | tf_op jit(solution)/shard_map/ppermute | solution.py:447
  23.2 0.7 copy-done.8
  23.9 1.1 right_stage.1
  25.0 16.4 %all-gather.1 = bf16[32,32,256]{2,1,0:T(8,128)(2,1)S(1)} all-gather(bf16[8,32,256]{2,1,0:T(8,128)(2,1)S(1)} %get-tuple-element.22), channel_id=3, replica_groups=mesh['y'=4,'zh'=4,'co'=2,'zl'=2,'x'=4] {'y'}, dimensions={0}, use_global_device_ids=true | all-gather | bytes 655360 | tf_op jit(solution)/shard_map/all_gather | solution.py:449
  41.4 1.2 copy-done.2
  42.6 0.9 copy-done.3
  43.6 0.7 copy-done.9
  44.3 0.7 copy-done.11
  44.9 13.5 %pair_stage.1 = (bf16[32,128,128]{2,1,0:T(8,128)(2,1)}, bf16[32,128,128]{2,1,0:T(8,128)(2,1)}, f32[32,8,128]{2,1,0:T(8,128)S(1)}) custom-call(bf16[4,8,32,256]{3,2,1,0:T(8,128)(2,1)S(1)} %bitcast.14, bf16[512,128]{1,0:T(8,128)(2,1)S(1)} %collective-permute-done.left_ref, bf16[32,128,128]{2,1,0:T(8,128)(2,1)S(1)} %copy-done.2, ...), custom_call_target="tpu_custom_call" | custom-call | flops 8000000000 | bytes 6000000 | tf_op jit(solution)/shard_map/pair_stage/pallas_call | solution.py:176
  58.5 8.9 %all-to-all-start = ((bf16[32,128,128]{2,1,0:T(8,128)(2,1)}), bf16[32,128,128]{2,1,0:T(8,128)(2,1)S(1)}, u32[]{:S(2)}, u32[]{:S(2)}) async-start(bf16[32,128,128]{2,1,0:T(8,128)(2,1)} %get-tuple-element.25), calls=%async_computation | async-start | bytes 2097152 | tf_op jit(solution)/shard_map/all_to_all | solution.py:459
  67.3 0.9 collective-permute-start.3
  68.2 0.8 collective-permute-start.2
  69.1 2.4 %collective-permute-start.1 = (bf16[8,128,128]{2,1,0:T(8,128)(2,1)S(1)}, bf16[8,128,128]{2,1,0:T(8,128)(2,1)S(1)}, u32[]{:S(2)}, u32[]{:S(2)}) collective-permute-start(bf16[8,128,128]{2,1,0:T(8,128)(2,1)S(1)} %get-tuple-element.27.refs_0_), channel_id=1, source_target_pairs={{0,64},{64,128},{128,192},{192,0},{1,65},{65,129},{129,193},{193,1... | collective-permute-start | bytes 786440 | tf_op jit(solution)/shard_map/ppermute | solution.py:452
  71.6 8.5 %collective-permute-done.3.refs_3_ = bf16[8,128,128]{2,1,0:T(8,128)(2,1)S(1)} collective-permute-done((bf16[8,128,128]{2,1,0:T(8,128)(2,1)S(1)}, bf16[8,128,128]{2,1,0:T(8,128)(2,1)S(1)}, u32[]{:S(2)}, u32[]{:S(2)}) %collective-permute-start.3) | collective-permute-done | bytes 262176 | tf_op jit(solution)/shard_map/ppermute | solution.py:452
  80.0 6.1 %collective-permute-done.2.refs_2_ = bf16[8,128,128]{2,1,0:T(8,128)(2,1)S(1)} collective-permute-done((bf16[8,128,128]{2,1,0:T(8,128)(2,1)S(1)}, bf16[8,128,128]{2,1,0:T(8,128)(2,1)S(1)}, u32[]{:S(2)}, u32[]{:S(2)}) %collective-permute-start.2) | collective-permute-done | bytes 262176 | tf_op jit(solution)/shard_map/ppermute | solution.py:452
  86.2 1.1 collective-permute-done.1.refs_1_
  87.2 4.3 %average_stage.1 = (bf16[2,544,128]{2,1,0:T(8,128)(2,1)S(1)}, bf16[2,544,128]{2,1,0:T(8,128)(2,1)S(1)}, bf16[2,544,128]{2,1,0:T(8,128)(2,1)S(1)}, bf16[2,544,128]{2,1,0:T(8,128)(2,1)S(1)}) custom-call(s32[3]{0:T(128)S(1)} %pad_add_fusion.me_ref, f32[32,8,128]{2,1,0:T(8,128)S(1)} %get-tuple-element.26.logit_ref, bf16[64,256]{1,0:T(8,128)(2,1)S(1)} %copy-done.5, ...), custom_call_target="tpu_custom_call" | custom-call | flops 2000000000 | bytes 3000000 | tf_op jit(solution)/shard_map/average_stage/pallas_call | solution.py:265
  91.6 0.1 collective-permute-start.4
  91.7 5.7 %collective-permute-start.5 = (bf16[2,544,128]{2,1,0:T(8,128)(2,1)S(1)}, bf16[2,544,128]{2,1,0:T(8,128)(2,1)S(1)}, u32[]{:S(2)}, u32[]{:S(2)}) collective-permute-start(bf16[2,544,128]{2,1,0:T(8,128)(2,1)S(1)} %get-tuple-element.30), channel_id=1, source_target_pairs={{0,2},{1,3},{2,0},{3,1},{4,6},{5,7},{6,4},{7,5},{8,10},{9,11},{10,... | collective-permute-start | bytes 835592 | tf_op jit(solution)/shard_map/ppermute | solution.py:463
  97.4 1.1 collective-permute-start.6
  98.5 4.1 %collective-permute-done.4.b_ref = bf16[2,544,128]{2,1,0:T(8,128)(2,1)S(1)} collective-permute-done((bf16[2,544,128]{2,1,0:T(8,128)(2,1)S(1)}, bf16[2,544,128]{2,1,0:T(8,128)(2,1)S(1)}, u32[]{:S(2)}, u32[]{:S(2)}) %collective-permute-start.4) | collective-permute-done | bytes 278560 | tf_op jit(solution)/shard_map/ppermute | solution.py:463
  102.5 6.8 %collective-permute-done.5.c_ref = bf16[2,544,128]{2,1,0:T(8,128)(2,1)S(1)} collective-permute-done((bf16[2,544,128]{2,1,0:T(8,128)(2,1)S(1)}, bf16[2,544,128]{2,1,0:T(8,128)(2,1)S(1)}, u32[]{:S(2)}, u32[]{:S(2)}) %collective-permute-start.5) | collective-permute-done | bytes 278560 | tf_op jit(solution)/shard_map/ppermute | solution.py:463
  109.3 0.7 merge_stage.1
  110.0 3.5 %collective-permute-start.7 = (bf16[544,128]{1,0:T(8,128)(2,1)S(1)}, bf16[544,128]{1,0:T(8,128)(2,1)S(1)}, u32[]{:S(2)}, u32[]{:S(2)}) collective-permute-start(bf16[544,128]{1,0:T(8,128)(2,1)S(1)} %get-tuple-element.33), channel_id=1, source_target_pairs={{0,4},{4,0},{1,5},{5,1},{2,6},{6,2},{3,7},{7,3},{8,12},{12,8},{9,1... | collective-permute-start | bytes 417800 | tf_op jit(solution)/shard_map/ppermute | solution.py:466
  113.5 2.8 %collective-permute-start.8 = (bf16[128,128]{1,0:T(8,128)(2,1)S(1)}, bf16[128,128]{1,0:T(8,128)(2,1)S(1)}, u32[]{:S(2)}, u32[]{:S(2)}) collective-permute-start(bf16[128,128]{1,0:T(8,128)(2,1)S(1)} %slice.9), channel_id=1, source_target_pairs={{0,0},{1,32},{2,64},{3,96},{4,128},{5,160},{6,192},{7,224},{8,1},{... | collective-permute-start | bytes 98312 | tf_op jit(solution)/shard_map/ppermute | solution.py:464
  116.2 11.5 %collective-permute-done.8.norm_ref = bf16[128,128]{1,0:T(8,128)(2,1)S(1)} collective-permute-done((bf16[128,128]{1,0:T(8,128)(2,1)S(1)}, bf16[128,128]{1,0:T(8,128)(2,1)S(1)}, u32[]{:S(2)}, u32[]{:S(2)}) %collective-permute-start.8) | collective-permute-done | bytes 32800 | tf_op jit(solution)/shard_map/ppermute | solution.py:464
  127.7 2.0 %combine_stage.1 = bf16[64,4,64]{2,1,0:T(4,128)(2,1)} custom-call(f32[544,128]{1,0:T(8,128)S(1)} %get-tuple-element.32.kept_ref, bf16[544,128]{1,0:T(8,128)(2,1)S(1)} %collective-permute-done.7.got_ref, bf16[128,128]{1,0:T(8,128)(2,1)S(1)} %collective-permute-done.8.norm_ref, bf16[64,256]{1,0:T(8,128)(2,1)S(1)} %copy-done.6, bf16[64,256]{1,0:T(8,128)(2,1)S(1)} %bitcast.16), custom_call_target="tpu_custom_call" | custom-call | flops 300000000 | bytes 2500000 | tf_op jit(solution)/shard_map/combine_stage/pallas_call | solution.py:365
  129.7 4.9 %triangle_stage.1 = (bf16[4,1024,512]{2,1,0:T(8,128)(2,1)}, bf16[4,4,1024]{2,1,0:T(4,128)(2,1)}) custom-call(bf16[32,128,128]{2,1,0:T(8,128)(2,1)S(1)} %all-to-all-done.turned_ref, bf16[128,512]{1,0:T(8,128)(2,1)S(1)} %copy-done.4, bf16[4,128]{1,0:T(4,128)(2,1)S(1)} %bitcast.19), custom_call_target="tpu_custom_call" | custom-call | flops 1000000000 | bytes 6000000 | tf_op jit(solution)/shard_map/triangle_stage/pallas_call | solution.py:390
  (24 shorter events, 0.1 us)
Async XLA Ops:
  0.6 0.8 copy-start
  1.5 0.7 copy-start.1
  20.2 21.3 %collective-permute-start = (bf16[512,128]{1,0:T(8,128)(2,1)S(1)}, bf16[512,128]{1,0:T(8,128)(2,1)S(1)}, u32[]{:S(2)}, u32[]{:S(2)}) collective-permute-start(bf16[512,128]{1,0:T(8,128)(2,1)S(1)} %bitcast.21), channel_id=1, source_target_pairs={{0,7},{8,1},{16,5},{24,4},{32,6},{40,3},{48,2},{56,0},{1,38},{9,32... | collective-permute-start | bytes 393224 | tf_op jit(solution)/shard_map/ppermute | solution.py:447
  23.2 0.7 copy-start.8
  41.4 1.2 copy-start.2
  42.6 0.9 copy-start.3
  43.6 0.7 copy-start.9
  44.3 0.7 copy-start.11
  44.9 42.3 %copy-start.5 = (bf16[64,256]{1,0:T(8,128)(2,1)S(1)}, bf16[64,256]{1,0:T(8,128)(2,1)}, u32[]{:S(2)}) copy-start(bf16[64,256]{1,0:T(8,128)(2,1)} %value_ref.1) | copy-start | bytes 98308
  58.5 71.3 %all-to-all-start = ((bf16[32,128,128]{2,1,0:T(8,128)(2,1)}), bf16[32,128,128]{2,1,0:T(8,128)(2,1)S(1)}, u32[]{:S(2)}, u32[]{:S(2)}) async-start(bf16[32,128,128]{2,1,0:T(8,128)(2,1)} %get-tuple-element.25), calls=%async_computation | async-start | bytes 2097152 | tf_op jit(solution)/shard_map/all_to_all | solution.py:459
  67.3 12.7 %collective-permute-start.3 = (bf16[8,128,128]{2,1,0:T(8,128)(2,1)S(1)}, bf16[8,128,128]{2,1,0:T(8,128)(2,1)S(1)}, u32[]{:S(2)}, u32[]{:S(2)}) collective-permute-start(bf16[8,128,128]{2,1,0:T(8,128)(2,1)S(1)} %get-tuple-element.27.refs_0_), channel_id=1, source_target_pairs={{0,192},{64,0},{128,64},{192,128},{1,193},{65,1},{129,65},{193,129... | collective-permute-start | bytes 786440 | tf_op jit(solution)/shard_map/ppermute | solution.py:452
  68.2 17.9 %collective-permute-start.2 = (bf16[8,128,128]{2,1,0:T(8,128)(2,1)S(1)}, bf16[8,128,128]{2,1,0:T(8,128)(2,1)S(1)}, u32[]{:S(2)}, u32[]{:S(2)}) collective-permute-start(bf16[8,128,128]{2,1,0:T(8,128)(2,1)S(1)} %get-tuple-element.27.refs_0_), channel_id=1, source_target_pairs={{0,128},{64,192},{128,0},{192,64},{1,129},{65,193},{129,1},{193,65... | collective-permute-start | bytes 786440 | tf_op jit(solution)/shard_map/ppermute | solution.py:452
  69.1 18.1 %collective-permute-start.1 = (bf16[8,128,128]{2,1,0:T(8,128)(2,1)S(1)}, bf16[8,128,128]{2,1,0:T(8,128)(2,1)S(1)}, u32[]{:S(2)}, u32[]{:S(2)}) collective-permute-start(bf16[8,128,128]{2,1,0:T(8,128)(2,1)S(1)} %get-tuple-element.27.refs_0_), channel_id=1, source_target_pairs={{0,64},{64,128},{128,192},{192,0},{1,65},{65,129},{129,193},{193,1... | collective-permute-start | bytes 786440 | tf_op jit(solution)/shard_map/ppermute | solution.py:452
  87.2 40.5 %copy-start.6 = (bf16[64,256]{1,0:T(8,128)(2,1)S(1)}, bf16[64,256]{1,0:T(8,128)(2,1)}, u32[]{:S(2)}) copy-start(bf16[64,256]{1,0:T(8,128)(2,1)} %gate_ref.1) | copy-start | bytes 98308
  87.2 40.5 %copy-start.7 = (bf16[256,64]{0,1:T(8,128)(2,1)S(1)}, bf16[256,64]{0,1:T(8,128)(2,1)}, u32[]{:S(2)}) copy-start(bf16[256,64]{0,1:T(8,128)(2,1)} %param.21) | copy-start | bytes 98308
  87.2 42.5 %copy-start.4 = (bf16[128,512]{1,0:T(8,128)(2,1)S(1)}, bf16[128,512]{1,0:T(8,128)(2,1)}, u32[]{:S(2)}) copy-start(bf16[128,512]{1,0:T(8,128)(2,1)} %proj_ref.3) | copy-start | bytes 393220
  87.2 42.5 %copy-start.10 = (bf16[128,4]{0,1:T(4,128)(2,1)S(1)}, bf16[128,4]{0,1:T(4,128)(2,1)}, u32[]{:S(2)}) copy-start(bf16[128,4]{0,1:T(4,128)(2,1)} %param.23) | copy-start | bytes 3076
  91.6 10.9 %collective-permute-start.4 = (bf16[2,544,128]{2,1,0:T(8,128)(2,1)S(1)}, bf16[2,544,128]{2,1,0:T(8,128)(2,1)S(1)}, u32[]{:S(2)}, u32[]{:S(2)}) collective-permute-start(bf16[2,544,128]{2,1,0:T(8,128)(2,1)S(1)} %get-tuple-element.29), channel_id=1, source_target_pairs={{0,1},{1,2},{2,3},{3,0},{4,5},{5,6},{6,7},{7,4},{8,9},{9,10},{10,1... | collective-permute-start | bytes 835592 | tf_op jit(solution)/shard_map/ppermute | solution.py:463
  91.7 17.6 %collective-permute-start.5 = (bf16[2,544,128]{2,1,0:T(8,128)(2,1)S(1)}, bf16[2,544,128]{2,1,0:T(8,128)(2,1)S(1)}, u32[]{:S(2)}, u32[]{:S(2)}) collective-permute-start(bf16[2,544,128]{2,1,0:T(8,128)(2,1)S(1)} %get-tuple-element.30), channel_id=1, source_target_pairs={{0,2},{1,3},{2,0},{3,1},{4,6},{5,7},{6,4},{7,5},{8,10},{9,11},{10,... | collective-permute-start | bytes 835592 | tf_op jit(solution)/shard_map/ppermute | solution.py:463
  97.4 11.9 %collective-permute-start.6 = (bf16[2,544,128]{2,1,0:T(8,128)(2,1)S(1)}, bf16[2,544,128]{2,1,0:T(8,128)(2,1)S(1)}, u32[]{:S(2)}, u32[]{:S(2)}) collective-permute-start(bf16[2,544,128]{2,1,0:T(8,128)(2,1)S(1)} %get-tuple-element.31), channel_id=1, source_target_pairs={{0,3},{1,0},{2,1},{3,2},{4,7},{5,4},{6,5},{7,6},{8,11},{9,8},{10,9... | collective-permute-start | bytes 835592 | tf_op jit(solution)/shard_map/ppermute | solution.py:463
  110.0 17.7 %collective-permute-start.7 = (bf16[544,128]{1,0:T(8,128)(2,1)S(1)}, bf16[544,128]{1,0:T(8,128)(2,1)S(1)}, u32[]{:S(2)}, u32[]{:S(2)}) collective-permute-start(bf16[544,128]{1,0:T(8,128)(2,1)S(1)} %get-tuple-element.33), channel_id=1, source_target_pairs={{0,4},{4,0},{1,5},{5,1},{2,6},{6,2},{3,7},{7,3},{8,12},{12,8},{9,1... | collective-permute-start | bytes 417800 | tf_op jit(solution)/shard_map/ppermute | solution.py:466
  113.5 14.2 %collective-permute-start.8 = (bf16[128,128]{1,0:T(8,128)(2,1)S(1)}, bf16[128,128]{1,0:T(8,128)(2,1)S(1)}, u32[]{:S(2)}, u32[]{:S(2)}) collective-permute-start(bf16[128,128]{1,0:T(8,128)(2,1)S(1)} %slice.9), channel_id=1, source_target_pairs={{0,0},{1,32},{2,64},{3,96},{4,128},{5,160},{6,192},{7,224},{8,1},{... | collective-permute-start | bytes 98312 | tf_op jit(solution)/shard_map/ppermute | solution.py:464
where the time goes:
time: 135 us
  waiting for transfers between devices  38 us (28%)
  blocking collectives  33.9 us (25%)
  starting transfers between devices  29.1 us (22%)
  Pallas kernels  27 us (20%)
  local copies, waits for them, and re-layouts  5.77 us (4%)
    all_gather x1, blocking collectives, per_device(): near = lax.all_gather(own, ('zh', 'co'), axis=0)  17.5 us
    all_gather x1, blocking collectives, per_device(): right = lax.all_gather(right, 'y', axis=0)  16.4 us
    ppermute x3, waiting for transfers between devices, per_device(): lax.ppermute(near_norm, 'y', [(c, (c + s) % 4) for c in range(4)])  15.7 us
    pallas_call x1, Pallas kernels, pair_stage(): pl.pallas_call(pair_kernel, grid=(steps,), in_specs=[pl.BlockSpec((4, 8,...  13.5 us
    ppermute x1, waiting for transfers between devices, per_device(): norm_own = lax.ppermute(own[:128], ALL, row_pairs())  11.5 us
    ppermute x3, waiting for transfers between devices, per_device(): moved[s] = lax.ppermute(parts[s], 'x', [(c, (c + s) % 4) for c in range(4)])  10.9 us
    all_to_all x1, starting transfers between devices, per_device(): turned = lax.all_to_all(turned, ROW, 0, 0, tiled=True)  8.88 us
    ppermute x3, starting transfers between devices, per_device(): moved[s] = lax.ppermute(parts[s], 'x', [(c, (c + s) % 4) for c in range(4)])  6.86 us
  transfers between devices with their start and end apart: 10, of which 6 were waited for; matrix products, arithmetic and copies ran while one was open for 0% of the time, Pallas kernels for 6%

commit v1 on v0

--- a/solution.py
+++ b/solution.py
@@ -50,7 +50,11 @@
     return jnp.where(here == there, tall, 0.0).astype(BF16)
 
 
-def prep_kernel(align_ref, left_ref, out_ref, wide, plane):
+def prep_kernel(
+    align_ref, left_ref, right_ref, logit_ref, out_ref, right_out, logit_out, wide, plane
+):
+    right_out[...] = right_ref[...]
+    logit_out[...] = logit_ref[...]
     wide[...] = align_ref[...].astype(F32)
     lefts = []
     for t in range(4):
@@ -63,15 +67,19 @@
     out_ref[128:192, :] = jnp.concatenate(lefts, axis=1).astype(BF16)
 
 
-def prep_stage(alignment, outer_left):
+def prep_stage(alignment, outer_left, outer_right, average_logit):
     return pl.pallas_call(
         prep_kernel,
-        out_shape=jax.ShapeDtypeStruct((192, 128), BF16),
+        out_shape=[
+            jax.ShapeDtypeStruct((192, 128), BF16),
+            jax.ShapeDtypeStruct((32, 64), BF16),
+            jax.ShapeDtypeStruct((8, 128), BF16),
+        ],
         scratch_shapes=[pltpu.VMEM((64, 4, 64), F32), pltpu.VMEM((64, 64), F32)],
         cost_estimate=cost(10_000_000, 100_000),
         compiler_params=pltpu.CompilerParams(vmem_limit_bytes=4 * 2**20),
         name="prep_stage",
-    )(alignment, outer_left)
+    )(alignment, outer_left, outer_right, average_logit)
 
 
 def right_kernel(near_ref, right_ref, out_ref, norm_ref, wide, tall):
@@ -150,7 +158,7 @@
                         axis=1,
                     )
                 )
-        update = dot(jnp.concatenate(outer_rows, axis=0), proj[...])
+        update = jnp.concatenate([dot(rows_i, proj[...]) for rows_i in outer_rows], axis=0)
         four = slice(quad * 4, (quad + 1) * 4)
         pair = pair_ref[four].reshape(512, 128).astype(F32)
         fresh = (pair + update * (1.0 / 64.0) + bias_ref[...]).astype(BF16)
@@ -374,11 +382,11 @@
 
 
 def triangle_kernel(turned_ref, proj_ref, bias_ref, inputs_ref, edge_ref, plane):
-    start = pl.program_id(0) * 4
-    plane[...] = turned_ref[pl.ds(start, 4)].reshape(512, 128).astype(F32)
+    start = pl.program_id(0) * 8
+    plane[...] = turned_ref[pl.ds(start, 8)].reshape(1024, 128).astype(F32)
     for q in range(4):
         rows = jnp.concatenate(
-            [plane[pl.ds(p * 128 + q, 32, stride=4), :] for p in range(4)], axis=0
+            [plane[pl.ds(p * 128 + q, 32, stride=4), :] for p in range(8)], axis=0
         ).astype(BF16)
         projected = dot(rows, proj_ref[...])
         inputs_ref[q, :, :384] = projected[:, :384].astype(BF16)
@@ -389,23 +397,23 @@
 def triangle_stage(turned, proj, bias):
     return pl.pallas_call(
         triangle_kernel,
-        grid=(8,),
+        grid=(4,),
         in_specs=[
             pl.BlockSpec(memory_space=pltpu.VMEM),
             pl.BlockSpec((128, 512), lambda b: (0, 0)),
             pl.BlockSpec((4, 128), lambda b: (0, 0)),
         ],
         out_specs=[
-            pl.BlockSpec((4, 128, 512), lambda b: (0, b, 0)),
-            pl.BlockSpec((4, 4, 128), lambda b: (0, 0, b)),
+            pl.BlockSpec((4, 256, 512), lambda b: (0, b, 0)),
+            pl.BlockSpec((4, 4, 256), lambda b: (0, 0, b)),
         ],
         out_shape=[
             jax.ShapeDtypeStruct((4, 1024, 512), BF16),
             jax.ShapeDtypeStruct((4, 4, 1024), BF16),
         ],
-        scratch_shapes=[pltpu.VMEM((512, 128), F32)],
+        scratch_shapes=[pltpu.VMEM((1024, 128), F32)],
         cost_estimate=cost(1_000_000_000, 6_000_000),
-        compiler_params=pltpu.CompilerParams(vmem_limit_bytes=10 * 2**20),
+        compiler_params=pltpu.CompilerParams(vmem_limit_bytes=14 * 2**20),
         name="triangle_stage",
     )(turned, proj, bias)
 
@@ -442,11 +450,14 @@
     average_value, average_gate, average_logit, average_out, triangle_proj, triangle_bias,
 ):
     me = jnp.stack([lax.axis_index(a) for a in ("y", "zl", "x")]).astype(jnp.int32)
-    own = prep_stage(alignment, jnp.transpose(outer_left))
+    own, right_w, logit_w = prep_stage(
+        alignment, jnp.transpose(outer_left), jnp.transpose(outer_right),
+        jnp.transpose(average_logit),
+    )
     near = lax.all_gather(own, ("zh", "co"), axis=0)
     left_rows = lax.ppermute(near[:, 128:].reshape(512, 128), ALL, left_pairs())
-    right, near_norm = right_stage(near, jnp.transpose(outer_right))
-    right = lax.all_gather(right, "y", axis=0)
+    right, near_norm = right_stage(near, right_w)
+    right = lax.all_to_all(jnp.broadcast_to(right[None], (4, 8, 32, 256)), "y", 0, 0, tiled=True)
     near_norm, right = lax.optimization_barrier((near_norm, right))
     norm_cols = [near_norm] + [
         lax.ppermute(near_norm, "y", [(c, (c + s) % 4) for c in range(4)])
@@ -454,7 +465,7 @@
     ]
     pair_new, turned, logits = pair_stage(
         right, left_rows, pair_rep, outer_proj,
-        outer_bias.reshape(1, 128), jnp.transpose(average_logit),
+        outer_bias.reshape(1, 128), logit_w,
     )
     turned = lax.all_to_all(turned, ROW, 0, 0, tiled=True)
     parts = average_stage(me, logits, average_value, norm_cols)
@@ -464,12 +475,13 @@
     norm_own = lax.ppermute(own[:128], ALL, row_pairs())
     kept, sent = merge_stage([parts[0], moved[1], moved[2], moved[3]])
     got = lax.ppermute(sent, "zl", [(0, 1), (1, 0)])
+    turned, kept = lax.optimization_barrier((turned, kept))
+    triangle_inputs, edge_bias = triangle_stage(
+        turned, triangle_proj, jnp.transpose(triangle_bias)
+    )
+    norm_own, edge_bias = lax.optimization_barrier((norm_own, edge_bias))
     alignment_update = combine_stage(
         kept, got, norm_own, average_gate, jnp.transpose(average_out)
-    )
-    turned, alignment_update = lax.optimization_barrier((turned, alignment_update))
-    triangle_inputs, edge_bias = triangle_stage(
-        turned, triangle_proj, jnp.transpose(triangle_bias)
     )
     return (pair_new, alignment_update, triangle_inputs, edge_bias)
 

time: 135 us -> 128 us (0.948)
  the two profiles are of different devices: /device:TPU:56 before, /device:TPU:198 now
where the time goes in v1:
time: 128 us
  waiting for transfers between devices  52.4 us (41%)
  starting transfers between devices  33.1 us (26%)
  Pallas kernels  22.6 us (18%)
  blocking collectives  14.8 us (12%)
  local copies, waits for them, and re-layouts  3.81 us (3%)
    ppermute x3, waiting for transfers between devices, per_device(): lax.ppermute(near_norm, 'y', [(c, (c + s) % 4) for c in range(4)])  22 us
    all_gather x1, blocking collectives, per_device(): near = lax.all_gather(own, ('zh', 'co'), axis=0)  14.8 us
    ppermute x3, waiting for transfers between devices, per_device(): moved[s] = lax.ppermute(parts[s], 'x', [(c, (c + s) % 4) for c in range(4)])  13.9 us
    all_to_all x1, starting transfers between devices, per_device(): turned = lax.all_to_all(turned, ROW, 0, 0, tiled=True)  12.3 us
    pallas_call x1, Pallas kernels, pair_stage(): pl.pallas_call(pair_kernel, grid=(steps,), in_specs=[pl.BlockSpec((4, 8,...  10.6 us
    ppermute x1, waiting for transfers between devices, per_device(): norm_own = lax.ppermute(own[:128], ALL, row_pairs())  7.31 us
    all_to_all x1, waiting for transfers between devices, per_device(): lax.all_to_all(jnp.broadcast_to(right[None], (4, 8, 32, 256)), 'y', 0, 0,...  6.12 us
    ppermute x3, starting transfers between devices, per_device(): lax.ppermute(near_norm, 'y', [(c, (c + s) % 4) for c in range(4)])  4.49 us
  transfers between devices with their start and end apart: 11, of which 8 were waited for; matrix products, arithmetic and copies ran while one was open for 0% of the time, Pallas kernels for 7%

profile of v1, /device:TPU:198, one launch (start us, length us, event | category | flops | bytes accessed | tf_op | source)
XLA Modules:
  0.0 127.6 jit_solution(16636630324151889739)
XLA Ops:
  0.7 0.8 copy-done
  1.5 0.7 copy-done.1
  2.2 0.7 copy-done.2
  2.9 0.7 copy-done.3
  3.6 0.5 prep_stage.1
  4.0 14.8 %all-gather = bf16[1536,128]{1,0:T(8,128)(2,1)S(1)} all-gather(bf16[192,128]{1,0:T(8,128)(2,1)S(1)} %get-tuple-element.26), channel_id=2, replica_groups=mesh['y'=4,'zh'=4,'co'=2,'zl'=2,'x'=4] {'zh','co'}, dimensions={0}, use_global_device_ids=true | all-gather | bytes 442368 | tf_op jit(solution)/shard_map/all_gather | solution.py:457
  18.8 1.1 right_stage.1
  20.0 0.9 broadcast_in_dim.2
  20.8 4.5 %all-to-all-start = ((bf16[4,8,32,256]{3,2,1,0:T(8,128)(2,1)}), bf16[4,8,32,256]{3,2,1,0:T(8,128)(2,1)S(1)}, u32[]{:S(2)}, u32[]{:S(2)}) async-start(bf16[4,8,32,256]{3,2,1,0:T(8,128)(2,1)} %broadcast_in_dim.2), calls=%async_computation | async-start | bytes 1048576 | tf_op jit(solution)/shard_map/all_to_all | solution.py:460
  25.3 4.4 %collective-permute-start = (bf16[512,128]{1,0:T(8,128)(2,1)S(1)}, bf16[512,128]{1,0:T(8,128)(2,1)S(1)}, u32[]{:S(2)}, u32[]{:S(2)}) collective-permute-start(bf16[512,128]{1,0:T(8,128)(2,1)S(1)} %bitcast.19), channel_id=1, source_target_pairs={{0,7},{8,1},{16,5},{24,4},{32,6},{40,3},{48,2},{56,0},{1,38},{9,32... | collective-permute-start | bytes 393224 | tf_op jit(solution)/shard_map/ppermute | solution.py:458
  29.7 6.1 %all-to-all-done.right_ref = bf16[4,8,32,256]{3,2,1,0:T(8,128)(2,1)S(1)} async-done(((bf16[4,8,32,256]{3,2,1,0:T(8,128)(2,1)}), bf16[4,8,32,256]{3,2,1,0:T(8,128)(2,1)S(1)}, u32[]{:S(2)}, u32[]{:S(2)}) %all-to-all-start) | async-done | bytes 524320 | tf_op jit(solution)/shard_map/all_to_all | solution.py:460
  35.8 3.1 %collective-permute-done.left_ref = bf16[512,128]{1,0:T(8,128)(2,1)S(1)} collective-permute-done((bf16[512,128]{1,0:T(8,128)(2,1)S(1)}, bf16[512,128]{1,0:T(8,128)(2,1)S(1)}, u32[]{:S(2)}, u32[]{:S(2)}) %collective-permute-start) | collective-permute-done | bytes 131104 | tf_op jit(solution)/shard_map/ppermute | solution.py:458
  38.9 10.6 %pair_stage.1 = (bf16[32,128,128]{2,1,0:T(8,128)(2,1)}, bf16[32,128,128]{2,1,0:T(8,128)(2,1)}, f32[32,8,128]{2,1,0:T(8,128)S(1)}) custom-call(bf16[4,8,32,256]{3,2,1,0:T(8,128)(2,1)S(1)} %all-to-all-done.right_ref, bf16[512,128]{1,0:T(8,128)(2,1)S(1)} %collective-permute-done.left_ref, bf16[32,128,128]{2,1,0:T(8,128)(2,1)S(1)} %copy-done.4, ...), custom_call_target="tpu_custom_call" | custom-call | flops 8000000000 | bytes 6000000 | tf_op jit(solution)/shard_map/pair_stage/pallas_call | solution.py:184
  49.5 12.3 %all-to-all-start.1 = ((bf16[32,128,128]{2,1,0:T(8,128)(2,1)}), bf16[32,128,128]{2,1,0:T(8,128)(2,1)S(1)}, u32[]{:S(2)}, u32[]{:S(2)}) async-start(bf16[32,128,128]{2,1,0:T(8,128)(2,1)} %get-tuple-element.33), calls=%async_computation.1 | async-start | bytes 2097152 | tf_op jit(solution)/shard_map/all_to_all | solution.py:470
  61.8 2.8 %collective-permute-start.3 = (bf16[8,128,128]{2,1,0:T(8,128)(2,1)S(1)}, bf16[8,128,128]{2,1,0:T(8,128)(2,1)S(1)}, u32[]{:S(2)}, u32[]{:S(2)}) collective-permute-start(bf16[8,128,128]{2,1,0:T(8,128)(2,1)S(1)} %get-tuple-element.35.refs_0_), channel_id=1, source_target_pairs={{0,192},{64,0},{128,64},{192,128},{1,193},{65,1},{129,65},{193,129... | collective-permute-start | bytes 786440 | tf_op jit(solution)/shard_map/ppermute | solution.py:463
  64.6 0.8 collective-permute-start.2
  65.4 0.9 collective-permute-start.1
  66.4 9.3 %collective-permute-done.3.refs_3_ = bf16[8,128,128]{2,1,0:T(8,128)(2,1)S(1)} collective-permute-done((bf16[8,128,128]{2,1,0:T(8,128)(2,1)S(1)}, bf16[8,128,128]{2,1,0:T(8,128)(2,1)S(1)}, u32[]{:S(2)}, u32[]{:S(2)}) %collective-permute-start.3) | collective-permute-done | bytes 262176 | tf_op jit(solution)/shard_map/ppermute | solution.py:463
  75.7 2.7 %collective-permute-done.2.refs_2_ = bf16[8,128,128]{2,1,0:T(8,128)(2,1)S(1)} collective-permute-done((bf16[8,128,128]{2,1,0:T(8,128)(2,1)S(1)}, bf16[8,128,128]{2,1,0:T(8,128)(2,1)S(1)}, u32[]{:S(2)}, u32[]{:S(2)}) %collective-permute-start.2) | collective-permute-done | bytes 262176 | tf_op jit(solution)/shard_map/ppermute | solution.py:463
  78.4 9.9 %collective-permute-done.1.refs_1_ = bf16[8,128,128]{2,1,0:T(8,128)(2,1)S(1)} collective-permute-done((bf16[8,128,128]{2,1,0:T(8,128)(2,1)S(1)}, bf16[8,128,128]{2,1,0:T(8,128)(2,1)S(1)}, u32[]{:S(2)}, u32[]{:S(2)}) %collective-permute-start.1) | collective-permute-done | bytes 262176 | tf_op jit(solution)/shard_map/ppermute | solution.py:463
  88.3 4.3 %average_stage.1 = (bf16[2,544,128]{2,1,0:T(8,128)(2,1)S(1)}, bf16[2,544,128]{2,1,0:T(8,128)(2,1)S(1)}, bf16[2,544,128]{2,1,0:T(8,128)(2,1)S(1)}, bf16[2,544,128]{2,1,0:T(8,128)(2,1)S(1)}) custom-call(s32[3]{0:T(128)S(1)} %pad_add_fusion.me_ref, f32[32,8,128]{2,1,0:T(8,128)S(1)} %get-tuple-element.34.logit_ref, bf16[64,256]{1,0:T(8,128)(2,1)S(1)} %copy-done.7, ...), custom_call_target="tpu_custom_call" | custom-call | flops 2000000000 | bytes 3000000 | tf_op jit(solution)/shard_map/average_stage/pallas_call | solution.py:273
  92.7 2.3 %collective-permute-start.4 = (bf16[2,544,128]{2,1,0:T(8,128)(2,1)S(1)}, bf16[2,544,128]{2,1,0:T(8,128)(2,1)S(1)}, u32[]{:S(2)}, u32[]{:S(2)}) collective-permute-start(bf16[2,544,128]{2,1,0:T(8,128)(2,1)S(1)} %get-tuple-element.37), channel_id=1, source_target_pairs={{0,1},{1,2},{2,3},{3,0},{4,5},{5,6},{6,7},{7,4},{8,9},{9,10},{10,1... | collective-permute-start | bytes 835592 | tf_op jit(solution)/shard_map/ppermute | solution.py:474
  95.0 0.8 collective-permute-start.5
  95.8 1.1 collective-permute-start.6
  96.9 10.2 %collective-permute-done.4.b_ref = bf16[2,544,128]{2,1,0:T(8,128)(2,1)S(1)} collective-permute-done((bf16[2,544,128]{2,1,0:T(8,128)(2,1)S(1)}, bf16[2,544,128]{2,1,0:T(8,128)(2,1)S(1)}, u32[]{:S(2)}, u32[]{:S(2)}) %collective-permute-start.4) | collective-permute-done | bytes 278560 | tf_op jit(solution)/shard_map/ppermute | solution.py:474
  107.2 3.7 %collective-permute-done.6.d_ref = bf16[2,544,128]{2,1,0:T(8,128)(2,1)S(1)} collective-permute-done((bf16[2,544,128]{2,1,0:T(8,128)(2,1)S(1)}, bf16[2,544,128]{2,1,0:T(8,128)(2,1)S(1)}, u32[]{:S(2)}, u32[]{:S(2)}) %collective-permute-start.6) | collective-permute-done | bytes 278560 | tf_op jit(solution)/shard_map/ppermute | solution.py:474
  110.9 0.7 merge_stage.1
  111.5 0.1 collective-permute-start.7
  111.6 3.2 %collective-permute-start.8 = (bf16[128,128]{1,0:T(8,128)(2,1)S(1)}, bf16[128,128]{1,0:T(8,128)(2,1)S(1)}, u32[]{:S(2)}, u32[]{:S(2)}) collective-permute-start(bf16[128,128]{1,0:T(8,128)(2,1)S(1)} %slice.7), channel_id=1, source_target_pairs={{0,0},{1,32},{2,64},{3,96},{4,128},{5,160},{6,192},{7,224},{8,1},{... | collective-permute-start | bytes 98312 | tf_op jit(solution)/shard_map/ppermute | solution.py:475
  114.8 3.4 %triangle_stage.1 = (bf16[4,1024,512]{2,1,0:T(8,128)(2,1)}, bf16[4,4,1024]{2,1,0:T(4,128)(2,1)}) custom-call(bf16[32,128,128]{2,1,0:T(8,128)(2,1)S(1)} %all-to-all-done.1.turned_ref, bf16[128,512]{1,0:T(8,128)(2,1)S(1)} %copy-done.6, bf16[4,128]{1,0:T(4,128)(2,1)S(1)} %bitcast.17), custom_call_target="tpu_custom_call" | custom-call | flops 1000000000 | bytes 6000000 | tf_op jit(solution)/shard_map/triangle_stage/pallas_call | solution.py:398
  118.3 7.3 %collective-permute-done.8.norm_ref = bf16[128,128]{1,0:T(8,128)(2,1)S(1)} collective-permute-done((bf16[128,128]{1,0:T(8,128)(2,1)S(1)}, bf16[128,128]{1,0:T(8,128)(2,1)S(1)}, u32[]{:S(2)}, u32[]{:S(2)}) %collective-permute-start.8) | collective-permute-done | bytes 32800 | tf_op jit(solution)/shard_map/ppermute | solution.py:475
  125.6 2.0 %combine_stage.1 = bf16[64,4,64]{2,1,0:T(4,128)(2,1)} custom-call(f32[544,128]{1,0:T(8,128)S(1)} %get-tuple-element.41.kept_ref, bf16[544,128]{1,0:T(8,128)(2,1)S(1)} %collective-permute-done.7.got_ref, bf16[128,128]{1,0:T(8,128)(2,1)S(1)} %collective-permute-done.8.norm_ref, bf16[64,256]{1,0:T(8,128)(2,1)S(1)} %copy-done.8, bf16[64,256]{1,0:T(8,128)(2,1)S(1)} %bitcast.16), custom_call_target="tpu_custom_call" | custom-call | flops 300000000 | bytes 2500000 | tf_op jit(solution)/shard_map/combine_stage/pallas_call | solution.py:373
  (26 shorter events, 0.1 us)
Async XLA Ops:
  0.6 38.3 %copy-start.11 = (f32[128]{0:T(128)S(1)}, f32[128]{0:T(128)}, u32[]{:S(2)}) copy-start(f32[128]{0:T(128)} %param.17) | copy-start | bytes 1540
  0.6 0.8 copy-start
  1.5 0.7 copy-start.1
  2.2 0.7 copy-start.2
  2.9 0.7 copy-start.3
  3.6 35.3 %copy-start.4 = (bf16[32,128,128]{2,1,0:T(8,128)(2,1)S(1)}, bf16[32,128,128]{2,1,0:T(8,128)(2,1)}, u32[]{:S(2)}) copy-start(bf16[32,128,128]{2,1,0:T(8,128)(2,1)} %pair_ref.1) | copy-start | bytes 3145732
  3.6 35.3 %copy-start.5 = (bf16[1024,128]{1,0:T(8,128)(2,1)S(1)}, bf16[1024,128]{1,0:T(8,128)(2,1)}, u32[]{:S(2)}) copy-start(bf16[1024,128]{1,0:T(8,128)(2,1)} %proj_ref.2) | copy-start | bytes 786436
  20.8 15.0 %all-to-all-start = ((bf16[4,8,32,256]{3,2,1,0:T(8,128)(2,1)}), bf16[4,8,32,256]{3,2,1,0:T(8,128)(2,1)S(1)}, u32[]{:S(2)}, u32[]{:S(2)}) async-start(bf16[4,8,32,256]{3,2,1,0:T(8,128)(2,1)} %broadcast_in_dim.2), calls=%async_computation | async-start | bytes 1048576 | tf_op jit(solution)/shard_map/all_to_all | solution.py:460
  25.3 13.6 %collective-permute-start = (bf16[512,128]{1,0:T(8,128)(2,1)S(1)}, bf16[512,128]{1,0:T(8,128)(2,1)S(1)}, u32[]{:S(2)}, u32[]{:S(2)}) collective-permute-start(bf16[512,128]{1,0:T(8,128)(2,1)S(1)} %bitcast.19), channel_id=1, source_target_pairs={{0,7},{8,1},{16,5},{24,4},{32,6},{40,3},{48,2},{56,0},{1,38},{9,32... | collective-permute-start | bytes 393224 | tf_op jit(solution)/shard_map/ppermute | solution.py:458
  38.9 49.4 %copy-start.7 = (bf16[64,256]{1,0:T(8,128)(2,1)S(1)}, bf16[64,256]{1,0:T(8,128)(2,1)}, u32[]{:S(2)}) copy-start(bf16[64,256]{1,0:T(8,128)(2,1)} %value_ref.1) | copy-start | bytes 98308
  49.5 65.3 %all-to-all-start.1 = ((bf16[32,128,128]{2,1,0:T(8,128)(2,1)}), bf16[32,128,128]{2,1,0:T(8,128)(2,1)S(1)}, u32[]{:S(2)}, u32[]{:S(2)}) async-start(bf16[32,128,128]{2,1,0:T(8,128)(2,1)} %get-tuple-element.33), calls=%async_computation.1 | async-start | bytes 2097152 | tf_op jit(solution)/shard_map/all_to_all | solution.py:470
  61.8 13.9 %collective-permute-start.3 = (bf16[8,128,128]{2,1,0:T(8,128)(2,1)S(1)}, bf16[8,128,128]{2,1,0:T(8,128)(2,1)S(1)}, u32[]{:S(2)}, u32[]{:S(2)}) collective-permute-start(bf16[8,128,128]{2,1,0:T(8,128)(2,1)S(1)} %get-tuple-element.35.refs_0_), channel_id=1, source_target_pairs={{0,192},{64,0},{128,64},{192,128},{1,193},{65,1},{129,65},{193,129... | collective-permute-start | bytes 786440 | tf_op jit(solution)/shard_map/ppermute | solution.py:463
  64.6 13.8 %collective-permute-start.2 = (bf16[8,128,128]{2,1,0:T(8,128)(2,1)S(1)}, bf16[8,128,128]{2,1,0:T(8,128)(2,1)S(1)}, u32[]{:S(2)}, u32[]{:S(2)}) collective-permute-start(bf16[8,128,128]{2,1,0:T(8,128)(2,1)S(1)} %get-tuple-element.35.refs_0_), channel_id=1, source_target_pairs={{0,128},{64,192},{128,0},{192,64},{1,129},{65,193},{129,1},{193,65... | collective-permute-start | bytes 786440 | tf_op jit(solution)/shard_map/ppermute | solution.py:463
  65.4 22.9 %collective-permute-start.1 = (bf16[8,128,128]{2,1,0:T(8,128)(2,1)S(1)}, bf16[8,128,128]{2,1,0:T(8,128)(2,1)S(1)}, u32[]{:S(2)}, u32[]{:S(2)}) collective-permute-start(bf16[8,128,128]{2,1,0:T(8,128)(2,1)S(1)} %get-tuple-element.35.refs_0_), channel_id=1, source_target_pairs={{0,64},{64,128},{128,192},{192,0},{1,65},{65,129},{129,193},{193,1... | collective-permute-start | bytes 786440 | tf_op jit(solution)/shard_map/ppermute | solution.py:463
  88.3 26.5 %copy-start.6 = (bf16[128,512]{1,0:T(8,128)(2,1)S(1)}, bf16[128,512]{1,0:T(8,128)(2,1)}, u32[]{:S(2)}) copy-start(bf16[128,512]{1,0:T(8,128)(2,1)} %proj_ref.3) | copy-start | bytes 393220
  88.3 26.5 %copy-start.10 = (bf16[128,4]{0,1:T(4,128)(2,1)S(1)}, bf16[128,4]{0,1:T(4,128)(2,1)}, u32[]{:S(2)}) copy-start(bf16[128,4]{0,1:T(4,128)(2,1)} %param.23) | copy-start | bytes 3076
  92.7 32.9 %copy-start.8 = (bf16[64,256]{1,0:T(8,128)(2,1)S(1)}, bf16[64,256]{1,0:T(8,128)(2,1)}, u32[]{:S(2)}) copy-start(bf16[64,256]{1,0:T(8,128)(2,1)} %gate_ref.1) | copy-start | bytes 98308
  92.7 32.9 %copy-start.9 = (bf16[256,64]{0,1:T(8,128)(2,1)S(1)}, bf16[256,64]{0,1:T(8,128)(2,1)}, u32[]{:S(2)}) copy-start(bf16[256,64]{0,1:T(8,128)(2,1)} %param.21) | copy-start | bytes 98308
  92.7 14.5 %collective-permute-start.4 = (bf16[2,544,128]{2,1,0:T(8,128)(2,1)S(1)}, bf16[2,544,128]{2,1,0:T(8,128)(2,1)S(1)}, u32[]{:S(2)}, u32[]{:S(2)}) collective-permute-start(bf16[2,544,128]{2,1,0:T(8,128)(2,1)S(1)} %get-tuple-element.37), channel_id=1, source_target_pairs={{0,1},{1,2},{2,3},{3,0},{4,5},{5,6},{6,7},{7,4},{8,9},{9,10},{10,1... | collective-permute-start | bytes 835592 | tf_op jit(solution)/shard_map/ppermute | solution.py:474
  95.0 12.2 %collective-permute-start.5 = (bf16[2,544,128]{2,1,0:T(8,128)(2,1)S(1)}, bf16[2,544,128]{2,1,0:T(8,128)(2,1)S(1)}, u32[]{:S(2)}, u32[]{:S(2)}) collective-permute-start(bf16[2,544,128]{2,1,0:T(8,128)(2,1)S(1)} %get-tuple-element.38), channel_id=1, source_target_pairs={{0,2},{1,3},{2,0},{3,1},{4,6},{5,7},{6,4},{7,5},{8,10},{9,11},{10,... | collective-permute-start | bytes 835592 | tf_op jit(solution)/shard_map/ppermute | solution.py:474
  95.8 15.0 %collective-permute-start.6 = (bf16[2,544,128]{2,1,0:T(8,128)(2,1)S(1)}, bf16[2,544,128]{2,1,0:T(8,128)(2,1)S(1)}, u32[]{:S(2)}, u32[]{:S(2)}) collective-permute-start(bf16[2,544,128]{2,1,0:T(8,128)(2,1)S(1)} %get-tuple-element.39), channel_id=1, source_target_pairs={{0,3},{1,0},{2,1},{3,2},{4,7},{5,4},{6,5},{7,6},{8,11},{9,8},{10,9... | collective-permute-start | bytes 835592 | tf_op jit(solution)/shard_map/ppermute | solution.py:474
  111.5 14.1 %collective-permute-start.7 = (bf16[544,128]{1,0:T(8,128)(2,1)S(1)}, bf16[544,128]{1,0:T(8,128)(2,1)S(1)}, u32[]{:S(2)}, u32[]{:S(2)}) collective-permute-start(bf16[544,128]{1,0:T(8,128)(2,1)S(1)} %get-tuple-element.42), channel_id=1, source_target_pairs={{0,4},{4,0},{1,5},{5,1},{2,6},{6,2},{3,7},{7,3},{8,12},{12,8},{9,1... | collective-permute-start | bytes 417800 | tf_op jit(solution)/shard_map/ppermute | solution.py:477
  111.6 13.9 %collective-permute-start.8 = (bf16[128,128]{1,0:T(8,128)(2,1)S(1)}, bf16[128,128]{1,0:T(8,128)(2,1)S(1)}, u32[]{:S(2)}, u32[]{:S(2)}) collective-permute-start(bf16[128,128]{1,0:T(8,128)(2,1)S(1)} %slice.7), channel_id=1, source_target_pairs={{0,0},{1,32},{2,64},{3,96},{4,128},{5,160},{6,192},{7,224},{8,1},{... | collective-permute-start | bytes 98312 | tf_op jit(solution)/shard_map/ppermute | solution.py:475
